TPU v7x, 32 devices: a whole 2x2x4 slice. The times are simulated.
32 devices in a mesh: box: 8 (over z, x), cone: 4 (over y, core).
Axes of the slice: x: 2, y: 2, z: 4, core: 2. Of those that a mesh axis runs over, the one named last changes fastest.
Arguments:
- leaf_factor: float32 [128, 96, 64, 64], P('box', 'cone'), may hold values from -0.6 to 0.6
- leaf_transfer: float32 [128, 96, 64, 64], P('box', 'cone'), may hold values from -0.5 to 0.5
- leaf_cone_map: int32 [96], P('cone'), may hold values from 0 to 95, as said below
- parent_transfer: float32 [16, 96, 64, 64], P('box', 'cone'), may hold values from -0.5 to 0.5
- parent_cone_map: int32 [96], P('cone'), may hold values from 0 to 95
- coupling: bfloat16 [16, 96, 8, 64, 64], P('box', 'cone'), may hold values from -6 to 6
- partner: int32 [16, 96, 8], P('box', 'cone'), may hold values from 0 to 15
- live: int32 [16, 96, 8], P('box', 'cone'), may hold values 0 or 1
Outputs:
- projected: bfloat16 [16, 96, 8, 64, 64], P('box', 'cone')
- new_transfer: float32 [16, 96, 64, 64], P('box', 'cone')
Inputs may be any that keep to these rules, and one draw needn't show every extreme that they name: leaf_cone_map[c] lies within 24 positions of c, counted cyclically modulo 96.
All inputs are finite; a program needn't handle non-finite values. No bound on the sum of `live` on one device may be relied on, other than what follows from the above.
Results may differ from a plain program's by a relative error of at most 0.001.
Values sent between devices are 32-bit elements; how exact they have to be, the bound alone decides.
A program may use at most 192 MiB of HBM per device.

v0:
```python
import jax
import jax.numpy as jnp
from jax import lax
from jax.sharding import PartitionSpec as P

HIGHEST = lax.Precision.HIGHEST


def with_halo(cells, sides, width):
    for axis, dim in sides:
        count = lax.axis_size(axis)
        head = lax.slice_in_dim(cells, 0, width, axis=dim)
        tail = lax.slice_in_dim(cells, cells.shape[dim] - width, cells.shape[dim], axis=dim)
        cells = jnp.concatenate(
            [
                lax.ppermute(tail, axis, [(i, (i + 1) % count) for i in range(count)]),
                cells,
                lax.ppermute(head, axis, [((i + 1) % count, i) for i in range(count)]),
            ],
            axis=dim,
        )
    return cells


def partner_2(value, axis, bit):
    mask = 2**bit
    pairs = [(source, source ^ mask) for source in range(lax.axis_size(axis))]
    return lax.ppermute(value, axis, pairs)


def gram_of(blocks):
    return jnp.einsum("bcji,bcjk->bcik", blocks, blocks, precision=HIGHEST)


def upper_factor(gram_sums):
    return jnp.swapaxes(jnp.linalg.cholesky(gram_sums), -1, -2)


def shards(
    leaf_factor,
    leaf_transfer,
    leaf_cone_map,
    parent_transfer,
    parent_cone_map,
    coupling,
    partner,
    live,
):
    rank_dim = leaf_factor.shape[-1]
    identity = jnp.eye(rank_dim, dtype=jnp.float32)
    factor = leaf_factor + identity
    local_cones = factor.shape[1]
    padded = with_halo(factor, (("cone", 1),), local_cones)
    all_cones = local_cones * lax.axis_size("cone")
    first_cone = lax.axis_index("cone") * local_cones
    position = (leaf_cone_map - first_cone + local_cones + all_cones) % all_cones
    matches = (position[:, None] == jnp.arange(3 * local_cones)[None, :]).astype(jnp.float32)
    chosen = jnp.einsum("cm,bmij->bcij", matches, padded, precision=HIGHEST)
    first_level = jnp.einsum("bcij,bcjk->bcik", chosen, leaf_transfer + identity, precision=HIGHEST)
    level_grams = gram_of(first_level)
    parents = level_grams.shape[0] // 8
    gram_one = level_grams.reshape((parents, 8) + level_grams.shape[1:]).sum(1) / 8.0
    upper_one = upper_factor(gram_one)
    segment = lax.all_gather(upper_one, "cone", axis=1, tiled=True)
    matches = (parent_cone_map[:, None] == jnp.arange(segment.shape[1])[None, :]).astype(
        jnp.float32
    )
    chosen_two = jnp.einsum("cm,bmij->bcij", matches, segment, precision=HIGHEST)
    second = jnp.einsum(
        "bcij,bcjk->bcik", chosen_two, parent_transfer + identity, precision=HIGHEST
    )
    own_gram = gram_of(second).sum(0)
    group_size = 8 // parents
    summed = own_gram
    for bit_index in range(group_size.bit_length() - 1):
        summed = summed + partner_2(summed, "box", bit_index)
    upper_two = upper_factor(summed / 8.0)
    spread = jnp.broadcast_to(upper_two[None], second.shape)
    solved = jax.scipy.linalg.solve_triangular(
        jnp.swapaxes(spread, -1, -2), jnp.swapaxes(second, -1, -2), lower=True
    )
    new_transfer = jnp.swapaxes(solved, -1, -2)
    left_side = jnp.einsum(
        "tcij,tcnjk->tcnik", upper_one, coupling.astype(jnp.float32), precision=HIGHEST
    )
    every_factor = lax.all_gather(upper_one, "box", axis=0, tiled=True)
    cone_ids = jnp.arange(upper_one.shape[1])
    partner_side = every_factor[partner, cone_ids[None, :, None]]
    whole_block = jnp.einsum("tcnij,tcnkj->tcnik", left_side, partner_side, precision=HIGHEST)
    projected = (whole_block * live[:, :, :, None, None].astype(jnp.float32)).astype(jnp.bfloat16)
    return (projected, new_transfer)


def solution(mesh):
    in_specs = (
        P("box", "cone", None, None),
        P("box", "cone", None, None),
        P("cone"),
        P("box", "cone", None, None),
        P("cone"),
        P("box", "cone", None, None, None),
        P("box", "cone", None),
        P("box", "cone", None),
    )
    out_specs = (P("box", "cone", None, None, None), P("box", "cone", None, None))
    return jax.shard_map(shards, mesh=mesh, in_specs=in_specs, out_specs=out_specs, check_vma=False)
```

profile of v0, /device:TPU:0, one launch (start us, length us, event | category | flops | bytes accessed | tf_op | source)
XLA Modules:
  0.0 1256.6 jit_solution(2560707372662970679)
XLA Ops:
  7.2 0.0 all-gather.5.cloned.1.call-start
  7.2 0.0 copy-start.4
  7.2 12.0 broadcast_add_fusion
  19.3 0.5 collective-permute-start
  19.8 1.9 collective-permute-start.1
  21.7 0.0 copy-done.4
  21.8 268.5 %collective-permute-done = f32[16,24,64,64]{3,2,1,0:T(8,128)} collective-permute-done((f32[16,24,64,64]{3,2,1,0:T(8,128)}, f32[16,24,64,64]{3,2,1,0:T(8,128)}, u32[]{:S(2)}, u32[]{:S(2)}) %collective-permute-start) | collective-permute-done | bytes 6291488 | tf_op jit(solution)/shard_map/ppermute | solution.py:16
  290.3 2.4 collective-permute-done.1
  292.7 24.9 %pad_maximum_fusion = f32[16,72,64,64]{3,2,1,0:T(8,128)} fusion(f32[16,24,64,64]{3,2,1,0:T(8,128)} %collective-permute-done.1, f32[16,24,64,64]{3,2,1,0:T(8,128)} %broadcast_add_fusion, f32[16,24,64,64]{3,2,1,0:T(8,128)} %collective-permute-done), kind=kLoop, calls=%fused_computation.1 | loop fusion | flops 9437184 | bytes 37748736 | tf_op jit(solution)/shard_map/concatenate | solution.py:14
  317.7 43.0 %fusion.10 = f32[16,24,64,64]{3,1,2,0:T(8,128)} fusion(f32[16,72,64,64]{3,2,1,0:T(8,128)} %pad_maximum_fusion, s32[24]{0:T(128)S(1)} %and_select_fusion), kind=kOutput, calls=%fused_computation.13 | convolution fusion | flops 1358956288 | bytes 25165920 | tf_op jit(solution)/shard_map/cm,bmij->bcij/dot_general | solution.py:58
  360.6 20.1 %fusion.4 = f32[16,24,64,64]{3,2,1,0:T(8,128)S(1)} fusion(f32[16,24,64,64]{3,1,2,0:T(8,128)} %fusion.10, f32[16,24,64,64]{3,2,1,0:T(8,128)} %param.9, f32[64,64]{1,0:T(8,128)S(1)} %fusion.33), kind=kOutput, calls=%fused_computation.7 | convolution fusion | flops 1209532416 | bytes 18890752 | tf_op jit(solution)/shard_map/bcij,bcjk->bcik/dot_general | solution.py:59
  380.8 21.8 %bitcast_reduce_fusion = f32[2,24,64,64]{3,2,1,0:T(8,128)S(1)} fusion(f32[16,24,64,64]{3,2,1,0:T(8,128)S(1)} %fusion.4), kind=kOutput, calls=%fused_computation.6 | convolution fusion | flops 1209335808 | bytes 7077888 | tf_op jit(solution)/shard_map/bcji,bcjk->bcik/dot_general | solution.py:32
  402.6 0.5 copy.93
  403.1 1.4 fusion.18
  404.5 291.6 %custom-call.12 = f32[2,24,64,64]{3,2,1,0:T(8,128)S(1)} custom-call(f32[2,24,64,64]{3,2,1,0:T(8,128)} %fusion.18), custom_call_target="Cholesky" | custom-call | tf_op jit(solution)/shard_map/jit(cholesky)/cholesky | solution.py:36
  696.1 0.2 select_reduce_fusion
  696.3 0.1 compare_reduce_fusion
  696.4 1.4 fusion.22
  697.8 0.0 all-gather.5.cloned.1.call-update
  697.8 0.0 all-gather.3.cloned.1.call-start
  697.9 3.1 copy.95
  701.0 0.0 all-gather.3.cloned.1.call-update
  701.0 0.0 copy-start.3
  701.0 45.0 %all-gather.5.cloned.1.call-done = f32[2,96,64,64]{2,3,1,0:T(8,128)} async-done(((f32[2,24,64,64]{2,3,1,0:T(8,128)}), f32[2,96,64,64]{2,3,1,0:T(8,128)}) %all-gather.5.cloned.1.call-update) | async-done | bytes 3145744 | tf_op jit(solution)/shard_map/all_gather | solution.py:64
  746.0 6.9 copy.98
  752.9 0.0 copy-done.3
  752.9 0.0 copy-start
  752.9 4.5 convolution_bitcast_fusion
  757.4 0.0 copy-done
  757.4 0.0 copy-start.1
  757.4 0.0 copy-start.2
  757.4 1.8 fusion.19
  759.3 3.6 convolution_bitcast_fusion.1
  762.9 1.4 collective-permute-start.2
  764.3 0.0 copy-done.1
  764.3 0.1 copy.96
  764.4 0.1 reshape.40
  764.5 0.0 copy-done.2
  764.5 0.1 copy.97
  764.6 29.1 %collective-permute-done.2 = f32[24,64,64]{1,2,0:T(8,128)} collective-permute-done((f32[24,64,64]{1,2,0:T(8,128)}, f32[24,64,64]{1,2,0:T(8,128)}, u32[]{:S(2)}, u32[]{:S(2)}) %collective-permute-start.2) | collective-permute-done | bytes 393248 | tf_op jit(solution)/shard_map/ppermute | solution.py:28
  793.7 1.5 add.81
  795.2 1.6 collective-permute-start.3
  796.7 10.0 fusion.13
  806.7 22.1 %collective-permute-done.3 = f32[24,64,64]{1,2,0:T(8,128)S(1)} collective-permute-done((f32[24,64,64]{1,2,0:T(8,128)S(1)}, f32[24,64,64]{1,2,0:T(8,128)S(1)}, u32[]{:S(2)}, u32[]{:S(2)}) %collective-permute-start.3) | collective-permute-done | bytes 393248 | tf_op jit(solution)/shard_map/ppermute | solution.py:28
  828.8 0.1 add_multiply_fusion
  828.9 0.3 copy.103
  829.2 1.0 fusion.23
  830.2 141.4 %custom-call.13 = f32[24,64,64]{2,1,0:T(8,128)S(1)} custom-call(f32[24,64,64]{2,1,0:T(8,128)} %fusion.23), custom_call_target="Cholesky" | custom-call | tf_op jit(solution)/shard_map/jit(cholesky)/cholesky | solution.py:36
  971.5 0.1 select_reduce_fusion.1
  971.7 0.1 compare_reduce_fusion.1
  971.8 0.1 select_bitcast_fusion
  971.9 0.2 fusion.17
  972.1 236.8 %custom-call.14 = f32[2,24,1,64,64]{3,4,2,1,0:T(8,128)} custom-call(f32[2,24,1,64,64]{4,3,2,1,0:T(8,128)S(1)} %fusion.17), custom_call_target="InvertDiagBlocksLowerTriangular" | custom-call | tf_op jit(solution)/shard_map/jit(_solve_triangular)/vmap(vmap())/triangular_solve | solution.py:79
  1209.0 4.2 fusion.15
  1213.2 0.0 all-gather.3.cloned.1.call-done
  1213.2 10.7 gather_fusion
  1223.9 25.5 %multiply_convert_fusion = bf16[2,24,8,64,64]{4,3,2,1,0:T(8,128)(2,1)} fusion(f32[2,24,8]{2,1,0:T(8,128)S(1)} %copy.97, f32[2,24,8,64,64]{4,3,2,1,0:T(8,128)} %bitcast.68, f32[2,24,64,8,64]{4,2,3,1,0:T(8,128)} %fusion.13), kind=kOutput, calls=%fused_computation.9 | convolution fusion | flops 1211105280 | bytes 15730176 | tf_op jit(solution)/shard_map/tcnij,tcnkj->tcnik/dot_general | solution.py:89
  (6 shorter events, 0.1 us)
Async XLA Ops:
  7.2 738.8 %all-gather.5.cloned.1.call-start = ((), (), s32[]{:S(2)}) async-start(), calls=%async_computation.1 | async-start | bytes 7864320 | tf_op jit(solution)/shard_map/all_gather | solution.py:64
  7.2 14.5 %copy-start.4 = (s32[24]{0:T(128)S(1)}, s32[24]{0:T(128)}, u32[]{:S(2)}) copy-start(s32[24]{0:T(128)} %param.10) | copy-start | bytes 292
  19.3 271.0 %collective-permute-start = (f32[16,24,64,64]{3,2,1,0:T(8,128)}, f32[16,24,64,64]{3,2,1,0:T(8,128)}, u32[]{:S(2)}, u32[]{:S(2)}) collective-permute-start(f32[16,24,64,64]{3,2,1,0:T(8,128)} %broadcast_add_fusion), channel_id=1, source_target_pairs={{0,1},{1,2},{2,3},{3,0},{4,5},{5,6},{6,7},{7,4},{8,9},{9,10},{10,1... | collective-permute-start | bytes 18874376 | tf_op jit(solution)/shard_map/ppermute | solution.py:16
  19.8 273.0 %collective-permute-start.1 = (f32[16,24,64,64]{3,2,1,0:T(8,128)}, f32[16,24,64,64]{3,2,1,0:T(8,128)}, u32[]{:S(2)}, u32[]{:S(2)}) collective-permute-start(f32[16,24,64,64]{3,2,1,0:T(8,128)} %broadcast_add_fusion), channel_id=1, source_target_pairs={{1,0},{2,1},{3,2},{0,3},{5,4},{6,5},{7,6},{4,7},{9,8},{10,9},{11,1... | collective-permute-start | bytes 18874376 | tf_op jit(solution)/shard_map/ppermute | solution.py:18
  697.8 515.4 %all-gather.3.cloned.1.call-start = ((), (), s32[]{:S(2)}) async-start(), calls=%async_computation | async-start | bytes 14155776 | tf_op jit(solution)/shard_map/all_gather | solution.py:86
  701.0 51.9 %copy-start.3 = (s32[24]{0:T(128)S(1)}, s32[24]{0:T(128)}, u32[]{:S(2)}) copy-start(s32[24]{0:T(128)} %param.12) | copy-start | bytes 292
  752.9 4.5 copy-start
  757.4 6.9 copy-start.1
  757.4 7.1 copy-start.2
  762.9 30.8 %collective-permute-start.2 = (f32[24,64,64]{1,2,0:T(8,128)}, f32[24,64,64]{1,2,0:T(8,128)}, u32[]{:S(2)}, u32[]{:S(2)}) collective-permute-start(f32[24,64,64]{1,2,0:T(8,128)} %convolution_bitcast_fusion.1), channel_id=1, source_target_pairs={{0,4},{4,0},{8,12},{12,8},{16,20},{20,16},{24,28},{28,24},{1,5},{5... | collective-permute-start | bytes 1179656 | tf_op jit(solution)/shard_map/ppermute | solution.py:28
  795.2 33.7 %collective-permute-start.3 = (f32[24,64,64]{1,2,0:T(8,128)S(1)}, f32[24,64,64]{1,2,0:T(8,128)S(1)}, u32[]{:S(2)}, u32[]{:S(2)}) collective-permute-start(f32[24,64,64]{1,2,0:T(8,128)S(1)} %add.81), channel_id=1, source_target_pairs={{0,8},{4,12},{8,0},{12,4},{16,24},{20,28},{24,16},{28,20},{1,9},{5... | collective-permute-start | bytes 1179656 | tf_op jit(solution)/shard_map/ppermute | solution.py:28
Sparse Core Ops, SparseCore 0:
  697.9 48.0 all-gather.4
  748.2 190.4 all-gather.2
where the time goes:
time: 1270 us; the launch traced here: 1260 us
  other arithmetic  713 us (56%)
  waiting for transfers between devices  367 us (29%)
  matrix products  135 us (11%)
  local copies, waits for them, and re-layouts  21.7 us (2%)
  between operations  14.6 us (1%)
    another operation x7, other arithmetic, upper_factor(): return jnp.swapaxes(jnp.linalg.cholesky(gram_sums), -1, -2)  434 us
    ppermute x1, waiting for transfers between devices, with_halo(): lax.ppermute(tail, axis, [(i, (i + 1) % count) for i in range(count)])  269 us
    another operation x2, other arithmetic, shards(): jax.scipy.linalg.solve_triangular(jnp.swapaxes(spread, -1, -2), jnp.swapa...  237 us
    ppermute x2, waiting for transfers between devices, partner_2(): return lax.ppermute(value, axis, pairs)  51.2 us
    all_gather x1, waiting for transfers between devices, shards(): segment = lax.all_gather(upper_one, 'cone', axis=1, tiled=True)  45 us
    dot_general x1, matrix products, shards(): chosen = jnp.einsum('cm,bmij->bcij', matches, padded, precision=HIGHEST)  43 us
    dot_general x1, matrix products, shards(): jnp.einsum('tcnij,tcnkj->tcnik', left_side, partner_side, precision=HIGHEST)  25.5 us
    dot_general x2, matrix products, gram_of(): return jnp.einsum('bcji,bcjk->bcik', blocks, blocks, precision=HIGHEST)  25.4 us
  transfers between devices with their start and end apart: 6, of which 5 were waited for; matrix products, arithmetic and copies ran while one was open for 33% of the time, Pallas kernels for 0%

commit v1 on v0

v1 whole, which is shorter than its diff:
```python
import functools

import jax
import jax.numpy as jnp
from jax import lax
from jax.experimental import pallas as pl
from jax.experimental.pallas import tpu as pltpu
from jax.sharding import PartitionSpec as P

HIGH = lax.Precision.HIGH
LEAVES = 8


def halves(value):
    top = value.astype(jnp.bfloat16)
    return top, (value - top.astype(jnp.float32)).astype(jnp.bfloat16)


def dot(a, b, dims):
    return lax.dot_general(a, b, (dims, ((), ())), preferred_element_type=jnp.float32)


def product(a, b, contract_b=0):
    a_top, a_low = halves(a)
    b_top, b_low = halves(b)
    dims = ((1,), (contract_b,))
    return dot(a_top, b_top, dims) + (dot(a_low, b_top, dims) + dot(a_top, b_low, dims))


def fold(block):
    half = block.shape[-2] // 2
    return jnp.concatenate([block[..., :half, :], block[..., half:, :]], axis=-1)


def unfold(block):
    half = block.shape[-1] // 2
    return jnp.concatenate([block[..., :half], block[..., half:]], axis=-2)


def gram_sum(rows):
    top, low = halves(rows)
    dims = ((0,), (0,))
    cross = dot(top, low, dims)
    return dot(top, top, dims) + (cross + cross.T)


def pack_kernel(picks_ref, factor_ref, out_ref):
    out_ref[...] = fold(factor_ref[...])


def pack(factor, picks):
    leaves, _, rank, _ = factor.shape
    count = picks.shape[0]
    return pl.pallas_call(
        pack_kernel,
        out_shape=jax.ShapeDtypeStruct((leaves, count, rank // 2, 2 * rank), factor.dtype),
        grid_spec=pltpu.PrefetchScalarGridSpec(
            num_scalar_prefetch=1,
            grid=(count,),
            in_specs=[pl.BlockSpec((leaves, 1, rank, rank), lambda k, picks: (0, picks[k], 0, 0))],
            out_specs=pl.BlockSpec((leaves, 1, rank // 2, 2 * rank), lambda k, picks: (0, k, 0, 0)),
        ),
        name="pack",
    )(picks, factor)


def identity_of(rank):
    rows = lax.broadcasted_iota(jnp.int32, (rank, rank), 0)
    columns = lax.broadcasted_iota(jnp.int32, (rank, rank), 1)
    return (rows == columns).astype(jnp.float32)


def leaf_kernel(side_ref, own_at, left_at, right_at, own_ref, left_ref, right_ref, move_ref, gram_ref, held, rows):
    c = pl.program_id(0)
    leaves, rank = held.shape[0], held.shape[-1]
    side = side_ref[c]

    @pl.when(side == 0)
    def _():
        held[...] = unfold(left_ref[:, 0])

    @pl.when(side == 1)
    def _():
        held[...] = own_ref[:, 0]

    @pl.when(side == 2)
    def _():
        held[...] = unfold(right_ref[:, 0])

    identity = identity_of(rank)
    for p in range(leaves // LEAVES):
        for leaf in range(LEAVES):
            at = p * LEAVES + leaf
            factor = held[at] + identity
            rows[p, pl.ds(leaf * rank, rank), :] = factor + product(factor, move_ref[at, 0])
        gram_ref[p, 0] = gram_sum(rows[p]) * (1.0 / LEAVES)


def leaf_grams(side, own_at, left_at, right_at, own, left, right, move):
    leaves, cones, rank, _ = own.shape
    parents = leaves // LEAVES
    whole = (leaves, 1, rank, rank)
    folded = (leaves, 1, rank // 2, 2 * rank)
    return pl.pallas_call(
        leaf_kernel,
        out_shape=jax.ShapeDtypeStruct((parents, cones, rank, rank), jnp.float32),
        grid_spec=pltpu.PrefetchScalarGridSpec(
            num_scalar_prefetch=4,
            grid=(cones,),
            in_specs=[
                pl.BlockSpec(whole, lambda c, s, o, l, r: (0, o[c], 0, 0)),
                pl.BlockSpec(folded, lambda c, s, o, l, r: (0, l[c], 0, 0)),
                pl.BlockSpec(folded, lambda c, s, o, l, r: (0, r[c], 0, 0)),
                pl.BlockSpec(whole, lambda c, s, o, l, r: (0, c, 0, 0)),
            ],
            out_specs=pl.BlockSpec((parents, 1, rank, rank), lambda c, s, o, l, r: (0, c, 0, 0)),
            scratch_shapes=[
                pltpu.VMEM((leaves, rank, rank), jnp.float32),
                pltpu.VMEM((parents, LEAVES * rank, rank), jnp.float32),
            ],
        ),
        name="leaf_grams",
    )(side, own_at, left_at, right_at, own, left, right, move)


def eliminate_kernel(inverse, gram_ref, upper_ref, *rest):
    if inverse:
        inverse_ref, work, solved = rest
    else:
        (work,) = rest
    rank, _, batch = gram_ref.shape
    work[...] = gram_ref[...]
    if inverse:
        shape = (rank, rank, batch)
        rows = lax.broadcasted_iota(jnp.int32, shape, 0)
        columns = lax.broadcasted_iota(jnp.int32, shape, 1)
        solved[...] = (rows == columns).astype(jnp.float32)
        inverse_ref[...] = jnp.zeros(shape, jnp.float32)
    tile = 8
    for block in range(rank // tile):
        low = block * tile
        width = rank - low
        if low:
            upper_ref[pl.ds(low, tile), pl.ds(0, low), :] = jnp.zeros((tile, low, batch), jnp.float32)

        def step(inner, carry, low=low, width=width):
            k = low + inner
            scale = 1.0 / jnp.sqrt(work[k, pl.ds(k, 1), :])
            places = low + lax.broadcasted_iota(jnp.int32, (width, batch), 0)
            row = jnp.where(places >= k, work[k, pl.ds(low, width), :] * scale, 0.0)
            upper_ref[k, pl.ds(low, width), :] = row
            if inverse:
                solved_row = solved[k, pl.ds(0, low + tile), :] * scale
                inverse_ref[k, pl.ds(0, low + tile), :] = solved_row
            for i in range(low, rank):
                weight = upper_ref[k, pl.ds(i, 1), :]
                start = (i // tile) * tile
                work[i, pl.ds(start, rank - start), :] = (
                    work[i, pl.ds(start, rank - start), :] - weight * row[start - low :]
                )
                if inverse:
                    solved[i, pl.ds(0, low + tile), :] = (
                        solved[i, pl.ds(0, low + tile), :] - weight * solved_row
                    )
            return carry

        lax.fori_loop(0, tile, step, 0)


def eliminate(grams, inverse):
    batch, rank, _ = grams.shape
    shape = jax.ShapeDtypeStruct((rank, rank, batch), jnp.float32)
    results = pl.pallas_call(
        functools.partial(eliminate_kernel, inverse),
        out_shape=[shape] * (1 + inverse),
        in_specs=[pl.BlockSpec(memory_space=pltpu.VMEM)],
        out_specs=[pl.BlockSpec(memory_space=pltpu.VMEM)] * (1 + inverse),
        scratch_shapes=[pltpu.VMEM(shape.shape, jnp.float32)] * (1 + inverse),
        name="eliminate",
    )(jnp.transpose(grams, (1, 2, 0)))
    return jnp.transpose(results[-1], (2, 0, 1))


def second_kernel(pick_ref, upper_ref, move_ref, second_ref, gram_ref, rows):
    parents, rank = move_ref.shape[0], move_ref.shape[-1]
    for p in range(parents):
        upper = unfold(upper_ref[0, p, 0])
        second = upper + product(upper, move_ref[p, 0])
        second_ref[p, 0] = second
        rows[pl.ds(p * rank, rank), :] = second
    gram_ref[0] = fold(gram_sum(rows[...]))


def second_level(picks, uppers, move):
    _, parents, cones, half, wide = uppers.shape
    rank = wide // 2
    whole = pl.BlockSpec((parents, 1, rank, rank), lambda c, picks: (0, c, 0, 0))
    return pl.pallas_call(
        second_kernel,
        out_shape=[
            jax.ShapeDtypeStruct(move.shape, jnp.float32),
            jax.ShapeDtypeStruct((cones, half, wide), jnp.float32),
        ],
        grid_spec=pltpu.PrefetchScalarGridSpec(
            num_scalar_prefetch=1,
            grid=(cones,),
            in_specs=[
                pl.BlockSpec(
                    (1, parents, 1, half, wide),
                    lambda c, picks: (picks[c] // cones, 0, picks[c] % cones, 0, 0),
                ),
                whole,
            ],
            out_specs=[whole, pl.BlockSpec((1, half, wide), lambda c, picks: (c, 0, 0))],
            scratch_shapes=[pltpu.VMEM((parents * rank, rank), jnp.float32)],
        ),
        name="second_level",
    )(picks, uppers, move)


def project_kernel(partner_ref, live_ref, own_ref, every_ref, coupling_ref, out_ref):
    c = pl.program_id(0)
    parents, slots = own_ref.shape[0], coupling_ref.shape[2]
    dims = ((1,), (0,))
    for t in range(parents):
        top, low = halves(unfold(own_ref[t, 0]))
        for j in range(slots):
            mate = unfold(every_ref[partner_ref[t, c, j], 0])
            block = coupling_ref[t, 0, j]
            left = dot(top, block, dims) + dot(low, block, dims)
            both = product(left, mate, 1)
            out_ref[t, 0, j] = (both * live_ref[t, c, j].astype(jnp.float32)).astype(out_ref.dtype)


def project(partner, live, own, every, coupling):
    parents, cones, slots, rank, _ = coupling.shape
    half, wide = own.shape[-2:]
    blocks = pl.BlockSpec((parents, 1, slots, rank, rank), lambda c, m, a: (0, c, 0, 0, 0))
    return pl.pallas_call(
        project_kernel,
        out_shape=jax.ShapeDtypeStruct(coupling.shape, coupling.dtype),
        grid_spec=pltpu.PrefetchScalarGridSpec(
            num_scalar_prefetch=2,
            grid=(cones,),
            in_specs=[
                pl.BlockSpec((parents, 1, half, wide), lambda c, m, a: (0, c, 0, 0)),
                pl.BlockSpec((every.shape[0], 1, half, wide), lambda c, m, a: (0, c, 0, 0)),
                blocks,
            ],
            out_specs=blocks,
        ),
        name="project",
    )(partner, live, own, every, coupling)


def partner_2(value, axis, bit):
    mask = 2**bit
    pairs = [(source, source ^ mask) for source in range(lax.axis_size(axis))]
    return lax.ppermute(value, axis, pairs)


def shards(
    leaf_factor,
    leaf_transfer,
    leaf_cone_map,
    parent_transfer,
    parent_cone_map,
    coupling,
    partner,
    live,
):
    leaves, cones, rank, _ = leaf_factor.shape
    parents = leaves // LEAVES
    count = lax.axis_size("cone")
    me = lax.axis_index("cone")

    maps = lax.all_gather(leaf_cone_map, "cone", axis=0, tiled=False)
    firsts = jnp.arange(count, dtype=jnp.int32)[:, None] * cones
    position = (maps - firsts + cones + count * cones) % (count * cones)
    side = position // cones
    place = position % cones
    is_side = (side[:, :, None] == jnp.arange(3)).astype(jnp.int32)
    order = jnp.cumsum(is_side, axis=1) - is_side
    slot = (order * is_side).sum(-1)
    busiest = jnp.maximum(is_side[..., 0].sum(1).max(), is_side[..., 2].sum(1).max())

    def listed(receiver, which, room):
        taken = (side[receiver] == which)[:, None] & (slot[receiver][:, None] == jnp.arange(room))
        return jnp.where(taken, place[receiver][:, None], 0).sum(0).astype(jnp.int32)

    def with_room(room):
        def run(factor, move):
            tail = pack(factor, listed((me + 1) % count, 0, room))
            head = pack(factor, listed((me + count - 1) % count, 2, room))
            left = lax.ppermute(tail, "cone", [(i, (i + 1) % count) for i in range(count)])
            right = lax.ppermute(head, "cone", [((i + 1) % count, i) for i in range(count)])
            mine, at = side[me], slot[me]
            return leaf_grams(
                mine,
                jnp.where(mine == 1, place[me], 0),
                jnp.where(mine == 0, at, 0),
                jnp.where(mine == 2, at, 0),
                factor,
                left,
                right,
                move,
            )

        return run

    room = (cones + 1) // 2
    gram_one = lax.cond(busiest <= room, with_room(room), with_room(cones), leaf_factor, leaf_transfer)

    upper_one = eliminate(gram_one.reshape((parents * cones, rank, rank)), False)
    upper_one = fold(upper_one).reshape((parents, cones, rank // 2, 2 * rank))
    segment = lax.all_gather(upper_one, "cone", axis=0, tiled=False)
    every_factor = lax.all_gather(upper_one, "box", axis=0, tiled=True)

    second, own_gram = second_level(parent_cone_map, segment, parent_transfer)
    group_size = LEAVES // parents
    summed = own_gram
    for bit_index in range(group_size.bit_length() - 1):
        summed = summed + partner_2(summed, "box", bit_index)
    inverse_two = eliminate(unfold(summed) / LEAVES, True)
    new_transfer = jnp.einsum("bcij,ckj->bcik", second, inverse_two, precision=HIGH)
    projected = project(partner, live, upper_one, every_factor, coupling)
    return (projected, new_transfer)


def solution(mesh):
    in_specs = (
        P("box", "cone", None, None),
        P("box", "cone", None, None),
        P("cone"),
        P("box", "cone", None, None),
        P("cone"),
        P("box", "cone", None, None, None),
        P("box", "cone", None),
        P("box", "cone", None),
    )
    out_specs = (P("box", "cone", None, None, None), P("box", "cone", None, None))
    return jax.shard_map(shards, mesh=mesh, in_specs=in_specs, out_specs=out_specs, check_vma=False)
```

time: 1270 us -> 328 us (0.26)
  other arithmetic: 713 us -> 7.79 us
  waiting for transfers between devices: 367 us -> 150 us
  matrix products: 135 us -> 3.8 us
  Pallas kernels: 0 us -> 125 us
    another operation x9 -> x1, other arithmetic: 671 us -> 0.07 us  [shards(): order = jnp.cumsum(is_side, axis=1) - is_side]
    ppermute x2, waiting for transfers between devices: 271 us -> 59.5 us  [the longest x1 49.8 us: run(): lax.ppermute(head, 'cone', [((i + 1) % count, i) for i in range(count)])]
    dot_general x8 -> x1, matrix products: 130 us -> 3.8 us  [shards(): jnp.einsum('bcij,ckj->bcik', second, inverse_two, precision=HIGH)]
    pallas_call x0 -> x7, Pallas kernels: none -> 125 us  [the longest x1 41 us: project(): pl.pallas_call(project_kernel, out_shape=jax.ShapeDtypeStruct(coupling.sh...]
    all_gather x1, waiting for transfers between devices: 0.01 us -> 38 us  [shards(): every_factor = lax.all_gather(upper_one, 'box', axis=0, tiled=True)]
    ppermute x2, waiting for transfers between devices: 51.2 us -> 22.5 us  [partner_2(): return lax.ppermute(value, axis, pairs)]
    concatenate x2, other arithmetic: 24.9 us -> 1.23 us  [the longest x1 1.16 us: fold(): jnp.concatenate([block[..., :half, :], block[..., half:, :]], axis=-1)]
    all_gather x1, waiting for transfers between devices: 45 us -> 29.4 us  [shards(): segment = lax.all_gather(upper_one, 'cone', axis=0, tiled=False)]
  transfers between devices with their start and end apart: 6 -> 6, of which waited for: 5 -> 6; matrix products, arithmetic and copies ran while one was open for 33% -> 4% of each run, Pallas kernels for 0% -> 12%
where the time goes in v1:
time: 328 us; the launch traced here: 326 us
  waiting for transfers between devices  150 us (46%)
  Pallas kernels  125 us (38%)
  between operations  16.1 us (5%)
  local copies, waits for them, and re-layouts  13.7 us (4%)
  other arithmetic  7.79 us (2%)
  blocking collectives  6.41 us (2%)
  matrix products  3.8 us (1%)
    ppermute x1, waiting for transfers between devices, run(): lax.ppermute(head, 'cone', [((i + 1) % count, i) for i in range(count)])  49.8 us
    pallas_call x1, Pallas kernels, project(): pl.pallas_call(project_kernel, out_shape=jax.ShapeDtypeStruct(coupling.sh...  41 us
    all_gather x1, waiting for transfers between devices, shards(): every_factor = lax.all_gather(upper_one, 'box', axis=0, tiled=True)  38 us
    all_gather x1, waiting for transfers between devices, shards(): segment = lax.all_gather(upper_one, 'cone', axis=0, tiled=False)  29.4 us
    pallas_call x1, Pallas kernels, leaf_grams(): pl.pallas_call(leaf_kernel, out_shape=jax.ShapeDtypeStruct((parents, cone...  28.2 us
    ppermute x2, waiting for transfers between devices, partner_2(): return lax.ppermute(value, axis, pairs)  22.5 us
    pallas_call x1, Pallas kernels, second_level(): pl.pallas_call(second_kernel, out_shape=[jax.ShapeDtypeStruct(move.shape,...  19.5 us
    pallas_call x2, Pallas kernels, eliminate(): pl.pallas_call(functools.partial(eliminate_kernel, inverse), out_shape=[s...  18.6 us
  transfers between devices with their start and end apart: 6, of which 6 were waited for; matrix products, arithmetic and copies ran while one was open for 4% of the time, Pallas kernels for 12%

profile of v1, /device:TPU:0, one launch (start us, length us, event | category | flops | bytes accessed | tf_op | source)
XLA Modules:
  0.0 325.9 jit_solution(15413607774483699934)
XLA Ops:
  7.2 0.0 all-gather.6.cloned.1.call-start
  7.2 1.2 dynamic-slice
  9.1 0.9 dynamic-update-slice
  10.0 6.4 %all-reduce = s32[96]{0:T(128)S(1)} all-reduce(s32[96]{0:T(128)S(1)} %dynamic-update-slice), channel_id=2, replica_groups=mesh['box'=8,'cone'=4] {'cone'}, use_global_device_ids=true, to_apply=%add | all-reduce | flops 96 | bytes 768
  16.4 0.1 reshape.54
  16.5 0.1 broadcast_compare_fusion
  16.6 0.1 copy.60
  16.7 0.1 slice_reduce_fusion
  16.9 0.1 reduce_window_sum.11
  16.9 0.6 reduce_max.18
  17.6 0.6 reduce_max.19
  19.5 107.7 %conditional.1 = (f32[2,24,64,64]{3,2,1,0:T(8,128)S(1)}) conditional(s32[]{:T(128)} %convert_element_type.7, (s32[]{:T(128)}, s32[4,24]{1,0:T(4,128)S(1)}, s32[4,24]{1,0:T(4,128)S(1)}, pred[4,24]{1,0:T(4,128)(4,1)S(1)}, s32[4,24]{1,0:T(4,128)S(1)}, /*index=5*/s32[4,24,3]{2,1,0:T(8,128)S(1)}, s32[4,24,3]{1,0,2:T(4,128)S(1)}, ...), branch_computations={%region_5.9_spmd, %region_9.13_spmd} | conditional | flops 5937 | bytes 50341540 | solution.py:312
  19.6 0.1 copy.62
  19.7 0.6 select_reduce_fusion.3.picks_ref
  20.4 8.9 %pack.7 = f32[16,12,32,128]{3,2,1,0:T(8,128)} custom-call(s32[12]{0:T(128)} %select_reduce_fusion.3.picks_ref, f32[16,24,64,64]{3,2,1,0:T(8,128)} %get-tuple-element.89.factor_ref.own_ref), custom_call_target="tpu_custom_call" | custom-call | tf_op jit(solution)/shard_map/cond/branch_1_fun/pack/pallas_call | solution.py:54
  29.3 0.0 collective-permute-start.3
  29.3 0.6 select_reduce_fusion.4.picks_ref
  29.9 8.4 %pack.6 = f32[16,12,32,128]{3,2,1,0:T(8,128)} custom-call(s32[12]{0:T(128)} %select_reduce_fusion.4.picks_ref, f32[16,24,64,64]{3,2,1,0:T(8,128)} %get-tuple-element.89.factor_ref.own_ref), custom_call_target="tpu_custom_call" | custom-call | tf_op jit(solution)/shard_map/cond/branch_1_fun/pack/pallas_call | solution.py:54
  38.3 0.0 collective-permute-start.2
  38.3 0.5 compare_select_fusion.3
  38.9 0.0 copy-start.4
  38.9 0.6 compare_select_fusion.4
  39.4 49.8 %collective-permute-done.3.right_ref = f32[16,12,32,128]{3,2,1,0:T(8,128)S(1)} collective-permute-done((f32[16,12,32,128]{3,2,1,0:T(8,128)}, f32[16,12,32,128]{3,2,1,0:T(8,128)S(1)}, u32[]{:S(2)}, u32[]{:S(2)}) %collective-permute-start.3) | collective-permute-done | bytes 3145760 | tf_op jit(solution)/shard_map/cond/branch_1_fun/ppermute | solution.py:296
  89.3 0.0 copy-start
  89.3 9.7 %collective-permute-done.2.left_ref = f32[16,12,32,128]{3,2,1,0:T(8,128)} collective-permute-done((f32[16,12,32,128]{3,2,1,0:T(8,128)}, f32[16,12,32,128]{3,2,1,0:T(8,128)}, u32[]{:S(2)}, u32[]{:S(2)}) %collective-permute-start.2) | collective-permute-done | bytes 3145760 | tf_op jit(solution)/shard_map/cond/branch_1_fun/ppermute | solution.py:295
  99.0 0.0 copy-done
  99.0 0.0 copy-done.4
  99.0 28.2 %leaf_grams.3 = f32[2,24,64,64]{3,2,1,0:T(8,128)S(1)} custom-call(s32[24]{0:T(128)} %copy-done.4, s32[24]{0:T(128)} %get-tuple-element.236.own_at, s32[24]{0:T(128)} %get-tuple-element.235.left_at, s32[24]{0:T(128)} %get-tuple-element.213.right_at, f32[16,24,64,64]{3,2,1,0:T(8,128)} %get-tuple-element.89.factor_ref.own_ref, ...), custom_call_target="tpu_custom_call" | custom-call | tf_op jit(solution)/shard_map/cond/branch_1_fun/leaf_grams/pallas_call | solution.py:104
  127.2 2.0 copy.63
  129.2 7.5 %eliminate.2 = f32[64,64,48]{2,1,0:T(8,128)} custom-call(f32[64,64,48]{2,1,0:T(8,128)} %bitcast.67), custom_call_target="tpu_custom_call" | custom-call | tf_op jit(solution)/shard_map/eliminate/pallas_call | solution.py:173
  136.7 1.7 fusion.27
  138.4 0.7 copy.64
  139.1 0.7 copy.65
  139.8 1.2 pad_maximum_fusion
  141.0 0.0 all-gather.6.cloned.1.call-update
  141.0 0.2 all-gather.4.cloned.1.call-start
  141.3 0.5 all-gather.4.cloned.1.call-update
  141.8 0.0 copy-start.1
  141.8 0.0 copy-start.2
  141.8 29.4 %all-gather.6.cloned.1.call-done.upper_ref = f32[4,2,24,32,128]{4,3,2,1,0:T(8,128)} async-done(((f32[1,2,24,32,128]{4,3,2,1,0:T(8,128)}), f32[4,2,24,32,128]{4,3,2,1,0:T(8,128)}) %all-gather.6.cloned.1.call-update) | async-done | bytes 3145744 | tf_op jit(solution)/shard_map/all_gather | solution.py:316
  171.2 19.5 %second_level.1 = (f32[2,24,64,64]{3,2,1,0:T(8,128)}, f32[24,32,128]{2,1,0:T(8,128)}) custom-call(s32[24]{0:T(128)} %pick_ref.1, f32[4,2,24,32,128]{4,3,2,1,0:T(8,128)} %all-gather.6.cloned.1.call-done.upper_ref, f32[2,24,64,64]{3,2,1,0:T(8,128)} %move_ref.1), custom_call_target="tpu_custom_call" | custom-call | tf_op jit(solution)/shard_map/second_level/pallas_call | solution.py:198
  190.7 1.4 collective-permute-start.4
  192.2 10.0 %collective-permute-done.4 = f32[24,32,128]{2,1,0:T(8,128)S(1)} collective-permute-done((f32[24,32,128]{2,1,0:T(8,128)}, f32[24,32,128]{2,1,0:T(8,128)S(1)}, u32[]{:S(2)}, u32[]{:S(2)}) %collective-permute-start.4) | collective-permute-done | bytes 393248 | tf_op jit(solution)/shard_map/ppermute | solution.py:259
  202.2 1.1 add.94
  203.2 1.5 collective-permute-start.5
  204.8 0.0 copy-done.1
  204.8 0.7 copy.66.partner_ref
  205.5 0.0 copy-done.2
  205.5 0.7 copy.67.live_ref
  206.1 12.5 %collective-permute-done.5 = f32[24,32,128]{2,1,0:T(8,128)S(1)} collective-permute-done((f32[24,32,128]{2,1,0:T(8,128)S(1)}, f32[24,32,128]{2,1,0:T(8,128)S(1)}, u32[]{:S(2)}, u32[]{:S(2)}) %collective-permute-start.5) | collective-permute-done | bytes 393248 | tf_op jit(solution)/shard_map/ppermute | solution.py:259
  218.6 0.1 add.95
  218.7 0.2 fusion.28
  218.9 0.1 pad_maximum_fusion.1
  219.0 0.7 copy.68
  219.6 1.5 multiply_bitcast_fusion.gram_ref
  221.1 11.1 %eliminate.3 = (f32[64,64,24]{2,1,0:T(8,128)}, f32[64,64,24]{2,1,0:T(8,128)}) custom-call(f32[64,64,24]{2,1,0:T(8,128)} %multiply_bitcast_fusion.gram_ref), custom_call_target="tpu_custom_call" | custom-call | tf_op jit(solution)/shard_map/eliminate/pallas_call | solution.py:173
  232.2 2.4 copy.73
  234.6 3.8 %fusion.20 = f32[2,24,64,64]{2,3,0,1:T(8,128)S(1)} fusion(f32[24,64,64,1]{2,1,3,0:T(8,128)S(1)} %copy.73, f32[2,24,64,64]{3,2,1,0:T(8,128)} %get-tuple-element.98), kind=kOutput, calls=%fused_computation.61 | convolution fusion | flops 75497472 | bytes 1966080 | tf_op jit(solution)/shard_map/bcij,ckj->bcik/dot_general | solution.py:325
  238.4 1.6 copy.72
  240.0 38.0 %all-gather.4.cloned.1.call-done.every_ref = f32[16,24,32,128]{3,2,1,0:T(8,128)} async-done(((f32[2,24,32,128]{3,2,1,0:T(8,128)}), f32[16,24,32,128]{3,2,1,0:T(8,128)}) %all-gather.4.cloned.1.call-update) | async-done | bytes 6291472 | tf_op jit(solution)/shard_map/all_gather | solution.py:317
  278.0 41.0 %project.1 = bf16[2,24,8,64,64]{4,3,2,1,0:T(8,128)(2,1)} custom-call(s32[2,24,8]{2,1,0:T(8,128)} %copy.66.partner_ref, s32[2,24,8]{2,1,0:T(8,128)} %copy.67.live_ref, f32[2,24,32,128]{3,2,1,0:T(8,128)} %bitcast.66, f32[16,24,32,128]{3,2,1,0:T(8,128)} %all-gather.4.cloned.1.call-done.every_ref, bf16[2,24,8,64,64]{4,3,2,1,0:T(8,128)(2,1)} %coupling_ref.1), custom_call_target="tpu_custom_call" | custom-call | tf_op jit(solution)/shard_map/project/pallas_call | solution.py:239
  (9 shorter events, 0.1 us)
Async XLA Ops:
  7.2 164.1 %all-gather.6.cloned.1.call-start = ((), (), s32[]{:S(2)}) async-start(), calls=%async_computation.1 | async-start | bytes 3932160 | tf_op jit(solution)/shard_map/all_gather | solution.py:316
  29.3 60.0 %collective-permute-start.3 = (f32[16,12,32,128]{3,2,1,0:T(8,128)}, f32[16,12,32,128]{3,2,1,0:T(8,128)S(1)}, u32[]{:S(2)}, u32[]{:S(2)}) collective-permute-start(f32[16,12,32,128]{3,2,1,0:T(8,128)} %pack.7), channel_id=1, source_target_pairs={{1,0},{2,1},{3,2},{0,3},{5,4},{6,5},{7,6},{4,7},{9,8},{10,9},{11,1... | collective-permute-start | bytes 9437192 | tf_op jit(solution)/shard_map/cond/branch_1_fun/ppermute | solution.py:296
  38.3 60.6 %collective-permute-start.2 = (f32[16,12,32,128]{3,2,1,0:T(8,128)}, f32[16,12,32,128]{3,2,1,0:T(8,128)}, u32[]{:S(2)}, u32[]{:S(2)}) collective-permute-start(f32[16,12,32,128]{3,2,1,0:T(8,128)} %pack.6), channel_id=1, source_target_pairs={{0,1},{1,2},{2,3},{3,0},{4,5},{5,6},{6,7},{7,4},{8,9},{9,10},{10,1... | collective-permute-start | bytes 9437192 | tf_op jit(solution)/shard_map/cond/branch_1_fun/ppermute | solution.py:295
  38.9 60.1 %copy-start.4 = (s32[24]{0:T(128)}, s32[24]{0:T(128)S(1)}, u32[]{:S(2)}) copy-start(s32[24]{0:T(128)S(1)} %get-tuple-element.214.side_ref) | copy-start | bytes 292 | tf_op jit(solution)/shard_map/cond
  89.3 9.7 %copy-start = (f32[16,12,32,128]{3,2,1,0:T(8,128)}, f32[16,12,32,128]{3,2,1,0:T(8,128)S(1)}, u32[]{:S(2)}) copy-start(f32[16,12,32,128]{3,2,1,0:T(8,128)S(1)} %collective-permute-done.3.right_ref) | copy-start | bytes 9437188 | tf_op jit(solution)/shard_map/cond
  141.0 137.0 %all-gather.4.cloned.1.call-start = ((), (), s32[]{:S(2)}) async-start(), calls=%async_computation | async-start | bytes 7077888 | tf_op jit(solution)/shard_map/all_gather | solution.py:317
  141.8 63.0 %copy-start.1 = (s32[2,24,8]{1,2,0:T(8,128)S(1)}, s32[2,24,8]{1,2,0:T(8,128)}, u32[]{:S(2)}) copy-start(s32[2,24,8]{1,2,0:T(8,128)} %param.16) | copy-start | bytes 4612
  141.8 63.7 %copy-start.2 = (s32[2,24,8]{1,2,0:T(8,128)S(1)}, s32[2,24,8]{1,2,0:T(8,128)}, u32[]{:S(2)}) copy-start(s32[2,24,8]{1,2,0:T(8,128)} %param.17) | copy-start | bytes 4612
  190.7 11.5 %collective-permute-start.4 = (f32[24,32,128]{2,1,0:T(8,128)}, f32[24,32,128]{2,1,0:T(8,128)S(1)}, u32[]{:S(2)}, u32[]{:S(2)}) collective-permute-start(f32[24,32,128]{2,1,0:T(8,128)} %get-tuple-element.96), channel_id=1, source_target_pairs={{0,4},{4,0},{8,12},{12,8},{16,20},{20,16},{24,28},{28,24},{1,5},{5... | collective-permute-start | bytes 1179656 | tf_op jit(solution)/shard_map/ppermute | solution.py:259
  203.2 15.4 %collective-permute-start.5 = (f32[24,32,128]{2,1,0:T(8,128)S(1)}, f32[24,32,128]{2,1,0:T(8,128)S(1)}, u32[]{:S(2)}, u32[]{:S(2)}) collective-permute-start(f32[24,32,128]{2,1,0:T(8,128)S(1)} %add.94), channel_id=1, source_target_pairs={{0,8},{4,12},{8,0},{12,4},{16,24},{20,28},{24,16},{28,20},{1,9},{5... | collective-permute-start | bytes 1179656 | tf_op jit(solution)/shard_map/ppermute | solution.py:259
Sparse Core Ops, SparseCore 0:
  141.2 30.0 all-gather.5
  173.4 104.5 all-gather.3
